TPU v7x, 512 devices: a 8x2x16 block of a 8x8x16 slice. The times are simulated.
512 devices in a mesh: frag: 2 (over y), band: 128 (over z, x), slab: 2 (over core).
Axes of the slice: x: 8, y: 2, z: 16, core: 2. Of those that a mesh axis runs over, the one named last changes fastest.
The devices are a block of a 8x8x16 slice.
Arguments:
- wavefunctions: bfloat16 [2048, 16384], P('band', ('frag', 'slab')), parts along dimension 1, may hold values from -6 to 6
- eigvec: bfloat16 [2048, 4096], P(None, ('frag', 'band', 'slab')), parts along dimension 1, may hold values from -1 to 1, as said below
- occupation: float32 [4096], P('frag'), parts along dimension 0, may hold values from 0.1 to 2
Outputs:
- rotated: float32 [2048, 16384], P('band', ('frag', 'slab')), parts along dimension 1
- density: float32 [16384], P(('frag', 'slab')), parts along dimension 0
There are 2 independent parts, one for each index of `frag`. A program takes and returns all parts, laid end to end along the dimension named above; each array names one. Nothing has to cross between parts.
Inputs may be any that keep to these rules, and one draw needn't show every extreme that they name: eigvec is an orthogonal matrix rounded to bfloat16.
All inputs are finite; a program needn't handle non-finite values.
Results may differ from a plain program's by a relative error of at most 0.0003.
Values may be sent and summed in bfloat16 or wider, within the bound.
No kernel may reach another device: no remote copies, remote signals or barrier semaphores. Data moves between devices by JAX's collectives and lax.ppermute only.
A program may use at most 64 MiB of HBM per device.

v0:
```python
import jax
import jax.numpy as jnp
from jax import lax
from jax.sharding import Mesh
from jax.sharding import PartitionSpec as P

BAND = ("band_0", "band_1")
BAND_SLAB = ("band_0", "band_1", "slab")
FRAG_BAND_SLAB = ("frag", "band_0", "band_1", "slab")


def in_blocks(array, dim, peers):
    dims = array.shape
    blocks = array.reshape(*dims[:dim], peers, dims[dim] // peers, *dims[dim + 1 :])
    return jnp.moveaxis(blocks, dim, 0)


def laid_out(blocks, dim):
    blocks = jnp.moveaxis(blocks, 0, dim)
    dims = blocks.shape
    return blocks.reshape(*dims[:dim], dims[dim] * dims[dim + 1], *dims[dim + 2 :])


def exchange_in_order(blocks, axes, turns):
    inside = blocks.shape[1:]
    result = blocks.reshape(*(lax.axis_size(a) for a in axes), *inside)
    for k in turns:
        result = lax.all_to_all(result, axes[k], k, k, tiled=True)
    return result.reshape(-1, *inside)


def one_axis_at_a_time(array, axes, turns, split_dim, concat_dim):
    blocks = in_blocks(array, split_dim, lax.axis_size(axes))
    return laid_out(exchange_in_order(blocks, axes, turns), concat_dim)


def stacked_from(array, axes, turns):
    blocks = array
    for k in turns:
        blocks = lax.all_gather(blocks, axes[k])
    done = turns[::-1]
    back = [done.index(k) for k in range(len(axes))]
    blocks = blocks.transpose(*back, *range(len(axes), blocks.ndim))
    return blocks.reshape(-1, *array.shape)


def whole_of(array, axes, turns, dim):
    return laid_out(stacked_from(array, axes, turns), dim)


def local(wavefunctions, eigvec, occupation):
    total_bands = eigvec.shape[0]
    by_points = one_axis_at_a_time(wavefunctions, BAND, (0, 1), 1, 0)
    point_rows = lax.dot_general(
        lax.all_gather(eigvec, BAND_SLAB, axis=1, tiled=True),
        by_points,
        (((0,), (0,)), ((), ())),
        preferred_element_type=jnp.float32,
    )
    rotated = lax.all_to_all(point_rows, BAND, split_axis=0, concat_axis=1, tiled=True)
    local_density = jnp.dot(
        occupation,
        point_rows * point_rows,
        precision=lax.Precision.HIGHEST,
        preferred_element_type=jnp.float32,
    ) / jnp.float32(total_bands)
    density = whole_of(local_density, BAND, (0, 1), 0)
    return (rotated, density)


def solution(mesh):
    torus = Mesh(
        mesh.devices.reshape(mesh.shape["frag"], 16, 8, mesh.shape["slab"]),
        ("frag", "band_0", "band_1", "slab"),
    )
    in_specs = (P(BAND, ("frag", "slab")), P(None, FRAG_BAND_SLAB), P("frag"))
    out_specs = (P(BAND, ("frag", "slab")), P(("frag", "slab")))
    return jax.shard_map(local, mesh=torus, in_specs=in_specs, out_specs=out_specs, check_vma=False)
```

profile of v0, /device:TPU:68, one launch (start us, length us, event | category | flops | bytes accessed | tf_op | source)
XLA Modules:
  0.0 287.4 jit_solution(17181273735163144986)
XLA Ops:
  7.2 0.0 copy-start
  7.2 0.1 all-gather.4.cloned.1.call-start
  7.3 0.7 all-gather.4.cloned.1.call-update
  8.0 1.3 reshape.13
  9.3 0.3 copy.18
  9.6 0.5 reshape.24
  10.2 58.1 %all_to_all.29 = bf16[16,2,2048]{2,1,0:T(2,128)(2,1)S(1)} all-to-all(bf16[16,2,2048]{2,1,0:T(2,128)(2,1)S(1)} %reshape.24), channel_id=1, replica_groups=mesh['frag'=2,'band_0'=16,'band_1'=8,'slab'=2] {'band_0'}, dimensions={0} | all-to-all | bytes 262144 | tf_op jit(solution)/shard_map/all_to_all | solution.py:28
  68.3 0.3 reshape.25
  68.6 0.5 reshape.26
  69.1 14.0 %all_to_all.30 = bf16[8,2,4096]{2,1,0:T(2,128)(2,1)S(1)} all-to-all(bf16[8,2,4096]{2,1,0:T(2,128)(2,1)S(1)} %reshape.26), channel_id=1, replica_groups=mesh['frag'=2,'band_0'=16,'band_1'=8,'slab'=2] {'band_1'}, dimensions={0} | all-to-all | bytes 262144 | tf_op jit(solution)/shard_map/all_to_all | solution.py:28
  83.1 0.3 reshape.27
  83.4 108.6 %all-gather.4.cloned.1.call-done = bf16[2048,2048]{0,1:T(8,128)(2,1)} async-done(((bf16[2048,8]{0,1:T(8,128)(2,1)}), bf16[2048,2048]{0,1:T(8,128)(2,1)}) %all-gather.4.cloned.1.call-update) | async-done | bytes 8388624 | tf_op jit(solution)/shard_map/all_gather | solution.py:55
  192.0 5.9 %fusion.2 = f32[2048,32]{0,1:T(8,128)S(1)} fusion(bf16[2048,2048]{0,1:T(8,128)(2,1)} %all-gather.4.cloned.1.call-done, bf16[2048,32]{1,0:T(8,128)(2,1)S(1)} %bitcast.25), kind=kOutput, calls=%fused_computation.4 | convolution fusion | flops 268435456 | bytes 8781824 | tf_op jit(solution)/shard_map/dot_general | solution.py:54
  197.9 0.3 copy.21
  198.3 1.2 reshape.28
  199.5 15.7 %all-to-all-start.2 = ((f32[128,1,512]{2,1,0:T(1,128)}), f32[128,1,512]{2,1,0:T(1,128)S(1)}, u32[]{:S(2)}, u32[]{:S(2)}) async-start(f32[128,1,512]{2,1,0:T(1,128)} %reshape.28), calls=%async_computation.2 | async-start | bytes 524288 | tf_op jit(solution)/shard_map/all_to_all | solution.py:60
  215.2 1.3 dynamic-slice
  217.1 0.0 copy-done
  217.1 0.3 fusion
  217.4 0.2 dynamic-update-slice
  217.6 32.8 %all-reduce = f32[512]{0:T(512)S(1)} all-reduce(f32[512]{0:T(512)S(1)} %dynamic-update-slice), channel_id=2, replica_groups=mesh['frag'=2,'band_0'=16,'band_1'=8,'slab'=2] {'band_0'}, use_global_device_ids=true, to_apply=%add | all-reduce | flops 512 | bytes 4096
  250.4 0.1 reshape.15
  250.5 25.8 %all-gather.1 = f32[128,32]{1,0:T(8,128)S(1)} all-gather(f32[16,32]{1,0:T(8,128)S(1)} %reshape.15), channel_id=3, replica_groups=mesh['frag'=2,'band_0'=16,'band_1'=8,'slab'=2] {'band_1'}, dimensions={0}, use_global_device_ids=true | all-gather | bytes 18432 | tf_op jit(solution)/shard_map/all_gather | solution.py:40
  276.3 0.7 reshape_reshape.7
  277.0 0.0 all-to-all-done.2
  277.0 0.5 broadcast.2
  277.5 1.3 reduce
  278.8 0.3 reshape.29
  279.0 0.3 copy.22
  279.4 1.2 all_to_all.25
  (4 shorter events, 0.1 us)
Async XLA Ops:
  7.2 209.9 %copy-start = (f32[2048]{0:T(1024)S(1)}, f32[2048]{0:T(1024)}, u32[]{:S(2)}) copy-start(f32[2048]{0:T(1024)} %param.5) | copy-start | bytes 24580
  7.2 184.8 %all-gather.4.cloned.1.call-start = ((), (), s32[]{:S(2)}) async-start(), calls=%async_computation.3 | async-start | bytes 8421376 | tf_op jit(solution)/shard_map/all_gather | solution.py:55
  199.5 77.5 %all-to-all-start.2 = ((f32[128,1,512]{2,1,0:T(1,128)}), f32[128,1,512]{2,1,0:T(1,128)S(1)}, u32[]{:S(2)}, u32[]{:S(2)}) async-start(f32[128,1,512]{2,1,0:T(1,128)} %reshape.28), calls=%async_computation.2 | async-start | bytes 524288 | tf_op jit(solution)/shard_map/all_to_all | solution.py:60
Sparse Core Ops, SparseCore 0:
  11.2 180.7 all-gather.3
where the time goes:
time: 288 us; the launch traced here: 287 us
  blocking collectives  131 us (45%)
  waiting for transfers between devices  109 us (38%)
  starting transfers between devices  15.8 us (5%)
  between operations  14.8 us (5%)
  local copies, waits for them, and re-layouts  9.42 us (3%)
  matrix products  6.21 us (2%)
    all_gather x1, waiting for transfers between devices, local(): lax.all_gather(eigvec, BAND_SLAB, axis=1, tiled=True)  109 us
    all_to_all x2, blocking collectives, exchange_in_order(): result = lax.all_to_all(result, axes[k], k, k, tiled=True)  72.1 us
    unnamed x1, blocking collectives  32.8 us
    all_gather x1, blocking collectives, stacked_from(): blocks = lax.all_gather(blocks, axes[k])  25.8 us
    all_to_all x1, starting transfers between devices, local(): lax.all_to_all(point_rows, BAND, split_axis=0, concat_axis=1, tiled=True)  15.7 us
    dot_general x1, matrix products, local(): lax.dot_general(lax.all_gather(eigvec, BAND_SLAB, axis=1, tiled=True), by...  5.94 us
  transfers between devices with their start and end apart: 2, of which 1 were waited for; matrix products, arithmetic and copies ran while one was open for 2% of the time, Pallas kernels for 0%

commit v1 on v0

--- a/solution.py
+++ b/solution.py
@@ -7,6 +7,13 @@
 BAND = ("band_0", "band_1")
 BAND_SLAB = ("band_0", "band_1", "slab")
 FRAG_BAND_SLAB = ("frag", "band_0", "band_1", "slab")
+
+
+def all_by_exchange(x, axis, dim):
+    n_dev = lax.axis_size(axis)
+    blocks = jnp.stack([x for _ in range(n_dev)])
+    blocks = lax.all_to_all(blocks, axis, split_axis=0, concat_axis=0)
+    return jnp.concatenate(blocks, axis=dim)
 
 
 def in_blocks(array, dim, peers):
@@ -52,7 +59,7 @@
     total_bands = eigvec.shape[0]
     by_points = one_axis_at_a_time(wavefunctions, BAND, (0, 1), 1, 0)
     point_rows = lax.dot_general(
-        lax.all_gather(eigvec, BAND_SLAB, axis=1, tiled=True),
+        all_by_exchange(eigvec, BAND_SLAB, 1),
         by_points,
         (((0,), (0,)), ((), ())),
         preferred_element_type=jnp.float32,

time: 288 us -> 547 us (1.90)
  the two profiles are of different devices: /device:TPU:68 before, /device:TPU:80 now
where the time goes in v1:
time: 547 us; the launch traced here: 546 us
  waiting for transfers between devices  359 us (66%)
  blocking collectives  130 us (24%)
  starting transfers between devices  33.8 us (6%)
  local copies, waits for them, and re-layouts  14.5 us (3%)
  matrix products  6.21 us (1%)
    all_to_all x1, waiting for transfers between devices, all_by_exchange(): blocks = lax.all_to_all(blocks, axis, split_axis=0, concat_axis=0)  359 us
    all_to_all x2, blocking collectives, exchange_in_order(): result = lax.all_to_all(result, axes[k], k, k, tiled=True)  74.3 us
    unnamed x1, blocking collectives  30.4 us
    all_gather x1, blocking collectives, stacked_from(): blocks = lax.all_gather(blocks, axes[k])  25.6 us
    all_to_all x1, starting transfers between devices, all_by_exchange(): blocks = lax.all_to_all(blocks, axis, split_axis=0, concat_axis=0)  17.7 us
    all_to_all x1, starting transfers between devices, local(): lax.all_to_all(point_rows, BAND, split_axis=0, concat_axis=1, tiled=True)  16.1 us
  transfers between devices with their start and end apart: 2, of which 1 were waited for; matrix products, arithmetic and copies ran while one was open for 1% of the time, Pallas kernels for 0%

profile of v1, /device:TPU:80, one launch (start us, length us, event | category | flops | bytes accessed | tf_op | source)
XLA Modules:
  0.0 546.4 jit_solution(7760398969740612055)
XLA Ops:
  0.6 0.0 copy-start
  0.6 1.3 reshape.23
  2.0 0.3 copy.19
  2.3 0.5 reshape.34
  2.8 58.1 %all_to_all.34 = bf16[16,2,2048]{2,1,0:T(2,128)(2,1)S(1)} all-to-all(bf16[16,2,2048]{2,1,0:T(2,128)(2,1)S(1)} %reshape.34), channel_id=1, replica_groups=mesh['frag'=2,'band_0'=16,'band_1'=8,'slab'=2] {'band_0'}, dimensions={0} | all-to-all | bytes 262144 | tf_op jit(solution)/shard_map/all_to_all | solution.py:35
  60.9 0.3 reshape.35
  61.2 0.5 reshape.36
  61.8 16.2 %all_to_all.35 = bf16[8,2,4096]{2,1,0:T(2,128)(2,1)S(1)} all-to-all(bf16[8,2,4096]{2,1,0:T(2,128)(2,1)S(1)} %reshape.36), channel_id=1, replica_groups=mesh['frag'=2,'band_0'=16,'band_1'=8,'slab'=2] {'band_1'}, dimensions={0} | all-to-all | bytes 262144 | tf_op jit(solution)/shard_map/all_to_all | solution.py:35
  78.0 5.0 stack.2
  83.0 17.7 %all-to-all-start = ((bf16[256,2048,8]{1,2,0:T(8,128)(2,1)}), bf16[256,2048,8]{1,2,0:T(8,128)(2,1)}, u32[]{:S(2)}, u32[]{:S(2)}) async-start(bf16[256,2048,8]{1,2,0:T(8,128)(2,1)} %stack.2), calls=%async_computation | async-start | bytes 16777216 | tf_op jit(solution)/shard_map/all_to_all | solution.py:15
  100.7 0.3 reshape.37
  101.0 358.9 %all-to-all-done = bf16[256,2048,8]{1,2,0:T(8,128)(2,1)} async-done(((bf16[256,2048,8]{1,2,0:T(8,128)(2,1)}), bf16[256,2048,8]{1,2,0:T(8,128)(2,1)}, u32[]{:S(2)}, u32[]{:S(2)}) %all-to-all-start) | async-done | bytes 8388640 | tf_op jit(solution)/shard_map/all_to_all | solution.py:15
  459.9 5.9 %fusion = f32[2048,32]{0,1:T(8,128)S(1)} fusion(bf16[2048,32]{1,0:T(8,128)(2,1)S(1)} %bitcast.29, bf16[256,2048,8]{1,2,0:T(8,128)(2,1)} %all-to-all-done), kind=kOutput, calls=%fused_computation | convolution fusion | flops 268435456 | bytes 8781824 | tf_op jit(solution)/shard_map/dot_general | solution.py:61
  465.9 0.3 copy.22
  466.2 1.2 reshape.38
  467.4 16.1 %all-to-all-start.3 = ((f32[128,1,512]{2,1,0:T(1,128)}), f32[128,1,512]{2,1,0:T(1,128)S(1)}, u32[]{:S(2)}, u32[]{:S(2)}) async-start(f32[128,1,512]{2,1,0:T(1,128)} %reshape.38), calls=%async_computation.3 | async-start | bytes 524288 | tf_op jit(solution)/shard_map/all_to_all | solution.py:67
  483.5 1.3 dynamic-slice
  485.4 0.0 copy-done
  485.4 0.3 fusion.2
  485.7 0.2 dynamic-update-slice
  485.9 30.4 %all-reduce = f32[512]{0:T(512)S(1)} all-reduce(f32[512]{0:T(512)S(1)} %dynamic-update-slice), channel_id=2, replica_groups=mesh['frag'=2,'band_0'=16,'band_1'=8,'slab'=2] {'band_0'}, use_global_device_ids=true, to_apply=%add | all-reduce | flops 512 | bytes 4096
  516.4 0.1 reshape.25
  516.4 25.6 %all-gather.1 = f32[128,32]{1,0:T(8,128)S(1)} all-gather(f32[16,32]{1,0:T(8,128)S(1)} %reshape.25), channel_id=3, replica_groups=mesh['frag'=2,'band_0'=16,'band_1'=8,'slab'=2] {'band_1'}, dimensions={0}, use_global_device_ids=true | all-gather | bytes 18432 | tf_op jit(solution)/shard_map/all_gather | solution.py:47
  542.1 0.7 reshape_reshape.7
  542.7 0.0 all-to-all-done.3
  542.7 0.5 broadcast.4
  543.3 1.3 reduce
  544.5 0.3 reshape.39
  544.8 0.3 copy.23
  545.2 1.2 all_to_all.29
  (4 shorter events, 0.1 us)
Async XLA Ops:
  0.6 484.8 %copy-start = (f32[2048]{0:T(1024)S(1)}, f32[2048]{0:T(1024)}, u32[]{:S(2)}) copy-start(f32[2048]{0:T(1024)} %param.5) | copy-start | bytes 24580
  83.0 377.0 %all-to-all-start = ((bf16[256,2048,8]{1,2,0:T(8,128)(2,1)}), bf16[256,2048,8]{1,2,0:T(8,128)(2,1)}, u32[]{:S(2)}, u32[]{:S(2)}) async-start(bf16[256,2048,8]{1,2,0:T(8,128)(2,1)} %stack.2), calls=%async_computation | async-start | bytes 16777216 | tf_op jit(solution)/shard_map/all_to_all | solution.py:15
  467.4 75.3 %all-to-all-start.3 = ((f32[128,1,512]{2,1,0:T(1,128)}), f32[128,1,512]{2,1,0:T(1,128)S(1)}, u32[]{:S(2)}, u32[]{:S(2)}) async-start(f32[128,1,512]{2,1,0:T(1,128)} %reshape.38), calls=%async_computation.3 | async-start | bytes 524288 | tf_op jit(solution)/shard_map/all_to_all | solution.py:67
